TPU v7x, 32 devices: a whole 2x2x4 slice. The times are simulated.
32 devices in a mesh: wide: 8 (over y, x, core), narrow: 4 (over z).
Axes of the slice: x: 2, y: 2, z: 4, core: 2. Of those that a mesh axis runs over, the one named last changes fastest.
Arguments:
- coefficients: float32 [8, 8192, 8192], P(None, 'wide', 'narrow'), may hold values from -0.07 to 0.07
- tensor_blocks: float32 [8, 32, 8192], P(None, 'wide', 'narrow'), may hold values from -6 to 6
- basis_rows: float32 [32, 8192], P(None, ('wide', 'narrow')), may hold values from -1.1 to 1.1, as said below
Outputs:
- new_basis: float32 [32, 8192], P(None, ('wide', 'narrow'))
- projection: float32 [32, 32], replicated
- factor: float32 [32, 32], replicated
Inputs may be any that keep to these rules, and one draw needn't show every extreme that they name: The rows of basis_rows are nearly but not exactly orthonormal: basis_rows basis_rows^T differs from the identity by less than 0.2 in spectral norm.
All inputs are finite; a program needn't handle non-finite values.
Results may differ from a plain program's by a relative error of at most 0.0002.
Values sent between devices are 32-bit elements; how exact they have to be, the bound alone decides.
A program may use at most 128 MiB of HBM per device.

v0:
```python
import jax
import jax.numpy as jnp
from jax import lax
from jax.sharding import PartitionSpec as P

N = 8192


def body(coefficients, tensor_blocks, basis_rows):
    hi = lax.Precision.HIGHEST
    partial_block = jnp.einsum(
        "kic,krc->ir",
        lax.all_gather(tensor_blocks, "wide", axis=1, tiled=True),
        coefficients,
        precision=hi,
    )
    image = lax.psum_scatter(partial_block, "narrow", scatter_dimension=1, tiled=True)
    local_first = jnp.dot(basis_rows, image.T, precision=hi)
    local_correlation = jnp.dot(basis_rows, basis_rows.T, precision=hi)
    first, correlation = lax.psum((local_first, local_correlation), ("wide", "narrow"))
    once = image - jnp.dot(first.T, basis_rows, precision=hi)
    second, raw_gram = lax.psum(
        (jnp.dot(basis_rows, once.T, precision=hi), jnp.dot(once, once.T, precision=hi)),
        ("wide", "narrow"),
    )
    twice = once - jnp.dot(second.T, basis_rows, precision=hi)
    cross = jnp.dot(second.T, second, precision=hi)
    weighted = jnp.dot(second.T, jnp.dot(correlation, second, precision=hi), precision=hi)
    gram = (raw_gram - 2.0 * cross + weighted) / N
    factor = jnp.linalg.cholesky(gram)
    new_basis = lax.linalg.triangular_solve(factor, twice, left_side=True, lower=True)
    return (new_basis, first + second, factor)


def solution(mesh):
    in_specs = (P(None, "wide", "narrow"), P(None, "wide", "narrow"), P(None, ("wide", "narrow")))
    out_specs = (P(None, ("wide", "narrow")), P(), P())
    return jax.shard_map(body, mesh=mesh, in_specs=in_specs, out_specs=out_specs, check_vma=False)
```

profile of v0, /device:TPU:0, one launch (start us, length us, event | category | flops | bytes accessed | tf_op | source)
XLA Modules:
  0.0 225.5 jit_solution(1987830653347588551)
XLA Ops:
  7.2 0.0 copy-start
  7.2 0.0 all-gather.2.cloned.1.call-start
  7.2 1.8 copy.11
  9.1 0.0 all-gather.2.cloned.1.call-update
  9.1 0.0 reduce-scatter.2.cloned.1.call-start
  9.1 31.3 %all-gather.2.cloned.1.call-done = f32[8,32,2048]{2,0,1:T(8,128)} async-done(((f32[8,4,2048]{2,0,1:T(8,128)}), f32[8,32,2048]{2,0,1:T(8,128)}) %all-gather.2.cloned.1.call-update) | async-done | bytes 2097168 | tf_op jit(solution)/shard_map/all_gather | solution.py:13
  40.4 67.1 %fusion.2 = f32[32,1024]{1,0:T(8,128)} fusion(f32[8,1024,2048]{2,1,0:T(8,128)} %param.3, f32[8,32,2048]{2,0,1:T(8,128)} %all-gather.2.cloned.1.call-done), kind=kOutput, calls=%fused_computation.2 | convolution fusion | flops 6442450944 | bytes 69337088 | tf_op jit(solution)/shard_map/kic,krc->ir/dot_general | solution.py:11
  107.5 0.0 reduce-scatter.2.cloned.1.call-update
  107.5 0.0 copy-done
  107.5 0.2 fusion.11
  107.7 19.4 %reduce-scatter.2.cloned.1.call-done = f32[32,256]{1,0:T(8,128)} async-done(((f32[32,1024]{1,0:T(8,128)}), f32[32,256]{1,0:T(8,128)}) %reduce-scatter.2.cloned.1.call-update) | async-done | bytes 32784 | tf_op jit(solution)/shard_map/reduce_scatter | solution.py:17
  127.1 0.9 convolution_bitcast_fusion.1
  128.1 38.5 %psum.28 = f32[32,32]{0,1:T(8,128)S(1)} all-reduce(f32[32,32]{0,1:T(8,128)S(1)} %convolution_bitcast_fusion.1), channel_id=1, replica_groups=mesh['wide'=8,'narrow'=4] {'wide','narrow'}, use_global_device_ids=true, to_apply=%region_1.0 | all-reduce | flops 1024 | bytes 8192 | tf_op jit(solution)/shard_map/psum | solution.py:20
  166.5 0.9 convolution_subtract_fusion.1
  167.4 0.2 convolution_bitcast_fusion
  167.6 0.2 fusion.10
  167.8 41.3 %all-reduce = (f32[32,32]{0,1:T(8,128)S(1)}, f32[32,32]{0,1:T(8,128)S(1)}, f32[32,32]{1,0:T(8,128)S(1)}) all-reduce(f32[32,32]{0,1:T(8,128)S(1)} %convolution_bitcast_fusion, f32[32,32]{0,1:T(8,128)S(1)} %fusion.10, f32[32,32]{1,0:T(8,128)S(1)} %fusion.11), channel_id=1, replica_groups=mesh['wide'=8,'narrow'=4] {'wide','narrow'}, use_global_device_ids=true, to_apply=%region_3.0 | all-reduce | flops 3072 | bytes 24576 | tf_op jit(solution)/shard_map/psum | solution.py:22
  209.1 0.2 convolution_subtract_fusion
  209.2 0.1 fusion.12
  209.4 0.2 fusion.6
  209.6 0.2 fusion.5
  209.8 0.1 copy.16
  209.9 2.9 %cholesky.16 = f32[32,32]{1,0:T(8,128)S(1)} custom-call(f32[32,32]{1,0:T(8,128)S(1)} %fusion.9), custom_call_target="Cholesky" | custom-call | tf_op jit(solution)/shard_map/jit(cholesky)/cholesky | solution.py:30
  212.8 0.6 compare_reduce_fusion
  213.5 1.3 select_bitcast_fusion
  214.7 2.4 %custom-call.6 = f32[1,32,32]{1,2,0:T(8,128)S(1)} custom-call(f32[1,32,32]{2,1,0:T(8,128)S(1)} %get-tuple-element.12), custom_call_target="InvertDiagBlocksLowerTriangular" | custom-call | tf_op jit(solution)/shard_map/triangular_solve | solution.py:31
  217.1 0.7 copy.17
  217.9 0.8 fusion.7
  (3 shorter events, 0.0 us)
Async XLA Ops:
  7.2 100.4 %copy-start = (f32[32,256]{1,0:T(8,128)S(1)}, f32[32,256]{1,0:T(8,128)}, u32[]{:S(2)}) copy-start(f32[32,256]{1,0:T(8,128)} %param.5) | copy-start | bytes 98308
  7.2 33.2 %all-gather.2.cloned.1.call-start = ((), (), s32[]{:S(2)}) async-start(), calls=%async_computation.1 | async-start | bytes 2359296 | tf_op jit(solution)/shard_map/all_gather | solution.py:13
  9.1 118.1 %reduce-scatter.2.cloned.1.call-start = ((), (), s32[]{:S(2)}) async-start(), calls=%async_computation.2 | async-start | bytes 163840 | tf_op jit(solution)/shard_map/reduce_scatter | solution.py:17
Sparse Core Ops, SparseCore 0:
  9.9 30.4 all-gather.1
  107.7 19.4 reduce-scatter.1
where the time goes:
time: 226 us
  blocking collectives  79.7 us (35%)
  matrix products  70.9 us (31%)
  waiting for transfers between devices  50.7 us (22%)
  between operations  14.1 us (6%)
  other arithmetic  7.3 us (3%)
  local copies, waits for them, and re-layouts  2.62 us (1%)
    dot_general x1, matrix products, body(): jnp.einsum('kic,krc->ir', lax.all_gather(tensor_blocks, 'wide', axis=1, t...  67.1 us
    psum x1, blocking collectives, body(): lax.psum((jnp.dot(basis_rows, once.T, precision=hi), jnp.dot(once, once.T...  41.3 us
    psum x1, blocking collectives, body(): lax.psum((local_first, local_correlation), ('wide', 'narrow'))  38.5 us
    all_gather x1, waiting for transfers between devices, body(): lax.all_gather(tensor_blocks, 'wide', axis=1, tiled=True)  31.3 us
    reduce_scatter x1, waiting for transfers between devices, body(): lax.psum_scatter(partial_block, 'narrow', scatter_dimension=1, tiled=True)  19.4 us
  transfers between devices with their start and end apart: 2, of which 2 were waited for; matrix products, arithmetic and copies ran while one was open for 0% of the time, Pallas kernels for 0%

commit v1 on v0

v1 whole, which is shorter than its diff:
```python
import functools

import jax
import jax.numpy as jnp
from jax import lax
from jax.experimental import pallas as pl
from jax.experimental.pallas import tpu as pltpu
from jax.sharding import PartitionSpec as P

MESH = pl.DeviceIdType.MESH
HI = lax.Precision.HIGHEST
F32 = jnp.float32
DEPTH = 4


def nt(a, b):
    return lax.dot_general(a, b, (((1,), (1,)), ((), ())), precision=HI, preferred_element_type=F32)


def nn(a, b):
    return lax.dot_general(a, b, (((1,), (0,)), ((), ())), precision=HI, preferred_element_type=F32)


def split(x):
    hi = x.astype(jnp.bfloat16)
    return hi, (x - hi.astype(F32)).astype(jnp.bfloat16)


def kernel(wide, narrow, total, coef, tens, basis, out_new, out_proj, out_fac,
           buf, tg, tf, ts, acc, bs, part, img, az1, aw1, az2, aw2,
           csem, lsem, t_send, t_recv, b_send, b_recv, r_send, r_recv,
           z1_send, z1_recv, w1_send, w1_recv, z2_send, z2_recv, w2_send, w2_recv):
    w = lax.axis_index("wide")
    n = lax.axis_index("narrow")
    terms, own, cols = tens.shape
    ranks = own * wide
    rows = basis.shape[1]
    half = wide // 2
    depth = min(DEPTH, terms)
    sib = w + 1 - 2 * lax.rem(w, 2)

    def peer(d):
        return lax.rem(w + 2 * d, wide)

    def sibpeer(d):
        return lax.rem(sib + 2 * d, wide)

    def zpeer(d):
        return lax.rem(n + d, narrow)

    def remote(src, dst, ss, rs, dev):
        return pltpu.make_async_remote_copy(
            src_ref=src, dst_ref=dst, send_sem=ss, recv_sem=rs, device_id=dev, device_id_type=MESH)

    def block(j):
        return lax.rem(n + 1 + j, narrow)

    def load(k, j):
        r0 = pl.multiple_of(block(j) * rows, rows)
        s = lax.rem(k, depth)
        return pltpu.make_async_copy(coef.at[k, pl.ds(r0, rows), :], buf.at[s, j], csem.at[s, j])

    local_t = pltpu.make_async_copy(tens, tg.at[:, w], lsem.at[0])
    local_b = pltpu.make_async_copy(basis, bs.at[n], lsem.at[1])
    local_t.start()
    local_b.start()
    for k in range(depth):
        for j in range(narrow):
            load(k, j).start()

    barrier = pltpu.get_barrier_semaphore()

    @pl.loop(1, wide)
    def _(d):
        pl.semaphore_signal(barrier, inc=1, device_id=(lax.rem(w + d, wide), n), device_id_type=MESH)

    for d in range(1, narrow):
        pl.semaphore_signal(barrier, inc=1, device_id=(w, zpeer(d)), device_id_type=MESH)
    pl.semaphore_wait(barrier, wide - 1 + narrow - 1)

    def t_out(k, d):
        return remote(tg.at[k, w], tg.at[k, w], t_send.at[k, d], t_recv.at[k, w], (peer(d), n))

    def t_sib(k):
        return remote(tg.at[k, w], tg.at[k, w], t_send.at[k, 0], t_recv.at[k, w], (sib, n))

    def t_fwd(k, d):
        p = peer(d)
        return remote(tg.at[k, p], tg.at[k, p], t_send.at[k, half + d], t_recv.at[k, p], (sib, n))

    def t_in(k, p):
        remote(tg.at[k, p], tg.at[k, p], t_send.at[k, 0], t_recv.at[k, p], (sib, n)).wait_recv()

    local_t.wait()

    @pl.loop(0, terms)
    def _(k):
        @pl.loop(1, half)
        def _(d):
            t_out(k, d).start()

        t_sib(k).start()

    local_b.wait()

    def b_out(d):
        return remote(bs.at[n], bs.at[n], b_send.at[d], b_recv.at[n], (w, zpeer(d)))

    for d in range(1, narrow):
        b_out(d).start()

    def forward(k):
        @pl.loop(1, half)
        def _(d):
            t_in(k, peer(d))
            t_fwd(k, d).start()

    def prepare(k):
        @pl.loop(0, half)
        def _(d):
            t_in(k, sibpeer(d))

        for q in range(wide):
            tf[q * own:(q + 1) * own, :] = tg[k, q]
        hi, lo = split(tf[...])
        ts[0:ranks, :] = hi
        ts[ranks:2 * ranks, :] = lo

    def product(s, j):
        hi, lo = split(buf[s, j])
        dims = (((1,), (1,)), ((), ()))
        t = ts[...]
        return (lax.dot_general(hi, t, dims, preferred_element_type=F32)
                + lax.dot_general(lo, t, dims, preferred_element_type=F32))

    acc[...] = jnp.zeros_like(acc)
    forward(0)

    @pl.loop(0, terms - 1)
    def _(k):
        s = lax.rem(k, depth)
        prepare(k)
        group = max(1, narrow // 2)
        for g in range(0, narrow, group):
            for j in range(g, g + group):
                load(k, j).wait()
            for j in range(g, g + group):
                acc[j] += product(s, j)
            for j in range(g, g + group):
                @pl.when(k + depth < terms)
                def _():
                    load(k + depth, j).start()
            if g == 0:
                forward(k + 1)

    last = terms - 1
    prepare(last)
    for d in range(1, narrow):
        q = zpeer(d)
        remote(bs.at[q], bs.at[q], b_send.at[d], b_recv.at[q], (w, q)).wait_recv()
    me = bs[n]
    corr = nt(me, me)

    def r_out(j):
        q = block(j)
        return remote(part.at[j], img.at[n], r_send.at[j], r_recv.at[n], (w, q))

    first_t = jnp.zeros((ranks, bs.shape[1]), F32)
    for j in range(narrow):
        load(last, j).wait()
        v = (acc[j] + product(last % depth, j)).T
        p = v[0:ranks] + v[ranks:2 * ranks]
        if j < narrow - 1:
            part[j] = p
            r_out(j).start()
        else:
            img[n] = p
        first_t = first_t + nt(p, bs[block(j)])

    def all_reduce(value, az, aw, zs, zr, ws, wr):
        az[n] = value

        def z_out(d):
            return remote(az.at[n], az.at[n], zs.at[d], zr.at[n], (w, zpeer(d)))

        for d in range(1, narrow):
            z_out(d).start()
        for d in range(1, narrow):
            q = zpeer(d)
            remote(az.at[q], az.at[q], zs.at[d], zr.at[q], (w, q)).wait_recv()
        t = az[0]
        for q in range(1, narrow):
            t = t + az[q]
        aw[w] = t

        def w_out(d):
            return remote(aw.at[w], aw.at[w], ws.at[d], wr.at[w], (lax.rem(w + d, wide), n))

        for d in range(1, wide):
            w_out(d).start()
        for d in range(1, wide):
            q = lax.rem(w + d, wide)
            remote(aw.at[q], aw.at[q], ws.at[d], wr.at[q], (q, n)).wait_recv()
        t = aw[0]
        for q in range(1, wide):
            t = t + aw[q]

        def finish():
            for d in range(1, narrow):
                z_out(d).wait_send()
            for d in range(1, wide):
                w_out(d).wait_send()

        return t, finish

    m = bs.shape[1]
    both, finish1 = all_reduce(jnp.concatenate([first_t, corr], axis=0), az1, aw1,
                               z1_send, z1_recv, w1_send, w1_recv)
    first_t = both[0:ranks]
    corr = both[ranks:ranks + m]
    proj_t = first_t + (first_t - nn(first_t, corr))
    for d in range(1, narrow):
        q = zpeer(d)
        remote(img.at[q], img.at[q], r_send.at[0], r_recv.at[q], (w, q)).wait_recv()
    image = img[0]
    for q in range(1, narrow):
        image = image + img[q]
    x = image - nn(proj_t, me)
    gram, finish2 = all_reduce(nt(x, x), az2, aw2, z2_send, z2_recv, w2_send, w2_recv)
    a = gram * (1.0 / total)
    sub = lax.broadcasted_iota(jnp.int32, (ranks, 1), 0)
    scale = jnp.ones((ranks, 1), F32)
    for j in range(ranks):
        rs = 1.0 / jnp.sqrt(a[j:j + 1, j:j + 1])
        lcol = jnp.where(sub > j, a[:, j:j + 1] * rs, 0.0)
        arow = a[j:j + 1, :] * rs
        xrow = x[j:j + 1, :] * rs
        scale = jnp.where(sub == j, rs, scale)
        a = a - lcol * arow
        x = x - lcol * xrow
    out_new[...] = x * scale
    upper = a * scale
    r_i = lax.broadcasted_iota(jnp.int32, (ranks, ranks), 0)
    c_i = lax.broadcasted_iota(jnp.int32, (ranks, ranks), 1)
    out_fac[...] = jnp.where(c_i >= r_i, upper, 0.0).T
    out_proj[...] = proj_t.T

    finish1()
    finish2()
    for j in range(narrow - 1):
        r_out(j).wait_send()
    for d in range(1, narrow):
        b_out(d).wait_send()

    @pl.loop(0, terms)
    def _(k):
        t_sib(k).wait_send()

        @pl.loop(1, half)
        def _(d):
            t_out(k, d).wait_send()
            t_fwd(k, d).wait_send()


def body(wide, narrow, total, coefficients, tensor_blocks, basis_rows):
    terms, own, cols = tensor_blocks.shape
    m, rows = basis_rows.shape
    ranks = own * wide
    depth = min(DEPTH, terms)
    dma = lambda *s: pltpu.SemaphoreType.DMA(s)
    vm = lambda s, t=F32: pltpu.VMEM(s, t)
    return pl.pallas_call(
        functools.partial(kernel, wide, narrow, total),
        out_shape=(
            jax.ShapeDtypeStruct((ranks, rows), F32),
            jax.ShapeDtypeStruct((m, ranks), F32),
            jax.ShapeDtypeStruct((ranks, ranks), F32),
        ),
        in_specs=[pl.BlockSpec(memory_space=pl.ANY)] * 3,
        out_specs=[pl.BlockSpec(memory_space=pltpu.VMEM)] * 3,
        scratch_shapes=[
            vm((depth, narrow, rows, cols)),
            vm((terms, wide, own, cols)),
            vm((ranks, cols)),
            vm((2 * ranks, cols), jnp.bfloat16),
            vm((narrow, rows, 2 * ranks)),
            vm((narrow, m, rows)),
            vm((narrow, ranks, rows)),
            vm((narrow, ranks, rows)),
            vm((narrow, ranks + m, m)),
            vm((wide, ranks + m, m)),
            vm((narrow, ranks, ranks)),
            vm((wide, ranks, ranks)),
            dma(depth, narrow), dma(2),
            dma(terms, wide), dma(terms, wide),
            dma(narrow), dma(narrow), dma(narrow), dma(narrow),
            dma(narrow), dma(narrow), dma(wide), dma(wide),
            dma(narrow), dma(narrow), dma(wide), dma(wide),
        ],
        compiler_params=pltpu.CompilerParams(
            collective_id=0, has_side_effects=True, vmem_limit_bytes=60 * 1024 * 1024),
        name="krylov_step",
    )(coefficients, tensor_blocks, basis_rows)


def solution(mesh):
    wide, narrow = mesh.shape["wide"], mesh.shape["narrow"]
    in_specs = (P(None, "wide", "narrow"), P(None, "wide", "narrow"), P(None, ("wide", "narrow")))
    out_specs = (P(None, ("wide", "narrow")), P(), P())

    def whole(coefficients, tensor_blocks, basis_rows):
        total = coefficients.shape[1]
        return jax.shard_map(functools.partial(body, wide, narrow, total), mesh=mesh,
                             in_specs=in_specs, out_specs=out_specs, check_vma=False)(
            coefficients, tensor_blocks, basis_rows)

    return whole
```

time: 226 us -> 68.9 us (0.30)
  blocking collectives: 79.7 us -> 0 us
  matrix products: 70.9 us -> 0 us
  Pallas kernels: 0 us -> 63.9 us
  waiting for transfers between devices: 50.7 us -> 0 us
  between operations: 14.1 us -> 0.64 us
  other arithmetic: 7.3 us -> 0 us
    psum x2 -> x0, blocking collectives: 79.7 us -> none  [the longest x1 41.3 us: body(): lax.psum((jnp.dot(basis_rows, once.T, precision=hi), jnp.dot(once, once.T...]
    dot_general x10 -> x0, matrix products: 70.1 us -> none  [the longest x1 67.1 us: body(): jnp.einsum('kic,krc->ir', lax.all_gather(tensor_blocks, 'wide', axis=1, t...]
    pallas_call x0 -> x1, Pallas kernels: none -> 63.9 us  [body(): pl.pallas_call(functools.partial(kernel, wide, narrow, total), out_shape=...]
    all_gather x1 -> x0, waiting for transfers between devices: 31.3 us -> none  [body(): lax.all_gather(tensor_blocks, 'wide', axis=1, tiled=True)]
    reduce_scatter x1 -> x0, waiting for transfers between devices: 19.4 us -> none  [body(): lax.psum_scatter(partial_block, 'narrow', scatter_dimension=1, tiled=True)]
    another operation x5 -> x0, other arithmetic: 7.29 us -> none  [the longest x2 3.69 us: body(): lax.linalg.triangular_solve(factor, twice, left_side=True, lower=True)]
  transfers between devices with their start and end apart: 2 -> 0, of which waited for: 2 -> 0; matrix products, arithmetic and copies ran while one was open for 0% -> 0% of each run, Pallas kernels for 0% -> 0%
where the time goes in v1:
time: 68.9 us; the launch traced here: 68.5 us
  Pallas kernels  63.9 us (93%)
  local copies, waits for them, and re-layouts  4.02 us (6%)
    pallas_call x1, Pallas kernels, body(): pl.pallas_call(functools.partial(kernel, wide, narrow, total), out_shape=...  63.9 us
    unnamed x3, local copies, waits for them, and re-layouts  4.02 us

profile of v1, /device:TPU:0, one launch (start us, length us, event | category | flops | bytes accessed | tf_op | source)
XLA Modules:
  0.0 68.5 jit_solution(10131767306988901224)
XLA Ops:
  0.6 63.9 %krylov_step.1 = (f32[32,256]{1,0:T(8,128)}, f32[32,32]{1,0:T(8,128)}, f32[32,32]{1,0:T(8,128)}) custom-call(f32[8,1024,2048]{2,1,0:T(8,128)} %coef.1, f32[8,4,2048]{2,1,0:T(4,128)} %tens.1, f32[32,256]{1,0:T(8,128)} %basis.1), custom_call_target="tpu_custom_call" | custom-call | tf_op jit(solution)/shard_map/krylov_step/pallas_call | solution.py:272
  64.5 1.4 %copy.9 = f32[32,256]{1,0:T(8,128)} copy(f32[32,256]{1,0:T(8,128)} %get-tuple-element.6) | data formatting | bytes 65536
  65.9 1.3 %copy.10 = f32[32,32]{1,0:T(8,128)} copy(f32[32,32]{1,0:T(8,128)} %get-tuple-element.7) | data formatting | bytes 8192
  67.2 1.3 %copy.11 = f32[32,32]{1,0:T(8,128)} copy(f32[32,32]{1,0:T(8,128)} %get-tuple-element.8) | data formatting | bytes 8192
